TPU v7x, 32 devices: a whole 2x2x4 slice. The times are simulated.
32 devices in a mesh: grp: 16 (over z, y, core), col: 2 (over x).
Axes of the slice: x: 2, y: 2, z: 4, core: 2. Of those that a mesh axis runs over, the one named last changes fastest.
Arguments:
- grad: float32 [4096, 16384], P('col', 'grp'), may hold values from -1.8 to 1.8
- exp_avg: float32 [4096, 16384], P('col', 'grp'), may hold values from -1.8 to 1.8
- exp_avg_sq: float32 [4096, 16384], P('col', 'grp'), may hold values from 0.01 to 0.36
- left_basis: bfloat16 [4096, 4096], P('grp', 'col'), may hold values from -1 to 1
- right_basis: bfloat16 [16384, 512], P('grp', 'col'), may hold values from -1 to 1
- gram_left: float32 [4096, 4096], P('grp', 'col'), may hold values from -6 to 6
- gram_right: float32 [16384, 512], P('grp', 'col'), may hold values from -6 to 6
Outputs:
- update: float32 [4096, 16384], P('col', 'grp')
- first_moment: float32 [4096, 16384], P('col', 'grp')
- second_moment: float32 [4096, 16384], P('col', 'grp')
- left_stat: float32 [4096, 4096], P('grp', 'col')
- right_stat: float32 [16384, 512], P('grp', 'col')
All inputs are finite; a program needn't handle non-finite values.
Results may differ from a plain program's by a relative error of at most 0.0041.
Values may be sent and summed in bfloat16 or wider, within the bound.
No kernel may reach another device: no remote copies, remote signals or barrier semaphores. Data moves between devices by JAX's collectives and lax.ppermute only.
A program may use at most 256 MiB of HBM per device.

v0:
```python
import jax
import jax.numpy as jnp
from jax import lax
from jax.sharding import PartitionSpec as P

RB = 512
decay = 0.95
bias_fix = 1.0 - decay**10


def local(grad, exp_avg, exp_avg_sq, left_basis, right_basis, gram_left, gram_right):
    col_count = lax.axis_size("col")
    rows_here, cols_here = grad.shape
    block_count = cols_here // RB
    rounded = grad.astype(jnp.bfloat16)
    panels = lax.all_gather(right_basis, "col", axis=1, tiled=True)
    blocks = panels.reshape(block_count, RB, RB)
    gathered = lax.all_gather(rounded, "col", axis=0, tiled=True)
    height = gathered.shape[0]
    product = jnp.einsum(
        "mbj,bjr->mbr",
        gathered.reshape(height, block_count, RB),
        blocks,
        preferred_element_type=jnp.float32,
    )
    turned = product.reshape(height, cols_here).astype(jnp.bfloat16)
    left_cols = lax.all_gather(left_basis, "grp", axis=0, tiled=True)
    rotated = lax.dot_general(
        left_cols, turned, (((0,), (0,)), ((), ())), preferred_element_type=jnp.float32
    )
    first_moment = decay * exp_avg + (1.0 - decay) * rotated
    second_moment = decay * exp_avg_sq + (1.0 - decay) * rotated * rotated
    direction = (first_moment / bias_fix / (jnp.sqrt(second_moment / bias_fix) + 1e-08)).astype(
        jnp.bfloat16
    )
    left_rows = lax.all_to_all(left_cols, "col", split_axis=0, concat_axis=1, tiled=True)
    back = jnp.dot(
        left_rows,
        lax.all_gather(direction, "col", axis=0, tiled=True),
        preferred_element_type=jnp.float32,
    )
    back = back.astype(jnp.bfloat16)
    update = jnp.einsum(
        "mbr,bjr->mbj",
        back.reshape(rows_here, block_count, RB),
        blocks,
        preferred_element_type=jnp.float32,
    )
    update = update.reshape(rows_here, cols_here)
    left_term = lax.psum_scatter(
        lax.dot_general(
            gathered, rounded, (((1,), (1,)), ((), ())), preferred_element_type=jnp.float32
        ),
        "grp",
        scatter_dimension=0,
        tiled=True,
    )
    left_stat = decay * gram_left + (1.0 - decay) * left_term
    share = RB // col_count
    offset = lax.axis_index("col") * share
    whole_blocks = gathered.reshape(gathered.shape[0], block_count, RB)
    narrow = lax.dynamic_slice_in_dim(whole_blocks, offset, share, 2)
    right_term = jnp.einsum(
        "mbj,mbr->bjr", whole_blocks, narrow, preferred_element_type=jnp.float32
    )
    right_stat = decay * gram_right + (1.0 - decay) * right_term.reshape(cols_here, share)
    return (update, first_moment, second_moment, left_stat, right_stat)


def solution(mesh):
    return jax.shard_map(
        local,
        mesh=mesh,
        in_specs=(
            P("col", "grp"),
            P("col", "grp"),
            P("col", "grp"),
            P("grp", "col"),
            P("grp", "col"),
            P("grp", "col"),
            P("grp", "col"),
        ),
        out_specs=(
            P("col", "grp"),
            P("col", "grp"),
            P("col", "grp"),
            P("grp", "col"),
            P("grp", "col"),
        ),
        check_vma=False,
    )
```

profile of v0, /device:TPU:0, one launch (start us, length us, event | category | flops | bytes accessed | tf_op | source)
XLA Modules:
  0.0 815.0 jit_solution(15229390837524339780)
XLA Ops:
  7.2 0.7 all-gather.5.cloned.1.call-update
  7.9 7.3 copy.32
  15.4 0.7 all-gather.9.cloned.1.call-update
  16.1 9.2 %copy.31 = f32[2048,1024]{0,1:T(8,128)} copy(f32[2048,1024]{1,0:T(8,128)} %param.8) | data formatting | bytes 16777216 | tf_op args[1]
  25.3 9.1 %copy.35 = f32[2048,1024]{0,1:T(8,128)} copy(f32[2048,1024]{1,0:T(8,128)} %param.9) | data formatting | bytes 16777216 | tf_op args[2]
  34.4 104.7 %all-gather.7.cloned.1.call-done = bf16[4096,1024]{0,1:T(8,128)(2,1)} async-done(((bf16[2048,1024]{0,1:T(8,128)(2,1)}), bf16[4096,1024]{0,1:T(8,128)(2,1)}) %all-gather.7.cloned.1.call-update) | async-done | bytes 8388624 | tf_op jit(solution)/shard_map/all_gather | solution.py:18
  139.1 12.1 %convolution_convert_fusion = bf16[2,512,4096]{2,1,0:T(8,128)(2,1)} fusion(bf16[2,512,512]{2,1,0:T(8,128)(2,1)} %bitcast.38, bf16[4096,2,512]{0,2,1:T(8,128)(2,1)} %bitcast.40), kind=kOutput, calls=%fused_computation.4 | convolution fusion | flops 4299161600 | bytes 17825792 | tf_op jit(solution)/shard_map/mbj,bjr->mbr/dot_general | solution.py:20
  151.2 116.5 %all-gather.9.cloned.1.call-done = bf16[4096,2048]{1,0:T(8,128)(2,1)} async-done(((bf16[256,2048]{1,0:T(8,128)(2,1)}), bf16[4096,2048]{1,0:T(8,128)(2,1)}) %all-gather.9.cloned.1.call-update) | async-done | bytes 16777232 | tf_op jit(solution)/shard_map/all_gather | solution.py:27
  267.7 33.8 %divide_convert_fusion = (bf16[2048,1024]{0,1:T(8,128)(2,1)}, f32[2048,1024]{0,1:T(8,128)}, f32[2048,1024]{0,1:T(8,128)}) fusion(f32[2048,1024]{0,1:T(8,128)} %copy.31, f32[2048,1024]{0,1:T(8,128)} %copy.35, bf16[4096,1024]{0,1:T(8,128)(2,1)} %bitcast.42, bf16[4096,2048]{1,0:T(8,128)(2,1)} %all-gather.9.cloned.1.call-done), kind=kOutput, calls=%fused_computation.3 | convolution fusion | flops 17202937856 | bytes 62914560 | tf_op jit(solution)/shard_map/dot_general | solution.py:28
  301.5 0.2 reduce-scatter.2.cloned.1.call-start
  301.7 25.6 %fusion.11 = f32[4096,2048]{1,0:T(8,128)} fusion(bf16[4096,1024]{0,1:T(8,128)(2,1)} %all-gather.7.cloned.1.call-done, bf16[2048,1024]{0,1:T(8,128)(2,1)} %copy.32), kind=kOutput, calls=%fused_computation.13 | convolution fusion | flops 17179869184 | bytes 46137344 | tf_op jit(solution)/shard_map/dot_general | solution.py:51
  327.3 9.7 %all-to-all-start = ((bf16[2,2048,2048]{2,1,0:T(8,128)(2,1)}), bf16[2,2048,2048]{2,1,0:T(8,128)(2,1)}, u32[]{:S(2)}, u32[]{:S(2)}) async-start(bf16[2,2048,2048]{2,1,0:T(8,128)(2,1)} %bitcast.35), calls=%async_computation | async-start | bytes 33554432 | tf_op jit(solution)/shard_map/all_to_all | solution.py:36
  337.1 7.1 fusion.6
  344.2 0.3 copy.39
  344.5 1.1 bitcast_add_fusion
  345.6 9.2 %copy.41 = f32[2048,1024]{1,0:T(8,128)} copy(f32[2048,1024]{0,1:T(8,128)} %get-tuple-element.21) | data formatting | bytes 16777216
  354.9 9.2 %copy.42 = f32[2048,1024]{1,0:T(8,128)} copy(f32[2048,1024]{0,1:T(8,128)} %get-tuple-element.22) | data formatting | bytes 16777216
  364.1 219.3 %all-to-all-done = bf16[2,2048,2048]{2,1,0:T(8,128)(2,1)} async-done(((bf16[2,2048,2048]{2,1,0:T(8,128)(2,1)}), bf16[2,2048,2048]{2,1,0:T(8,128)(2,1)}, u32[]{:S(2)}, u32[]{:S(2)}) %all-to-all-start) | async-done | bytes 16777248 | tf_op jit(solution)/shard_map/all_to_all | solution.py:36
  583.4 22.8 %copy.36 = bf16[2048,2,2048]{0,2,1:T(8,128)(2,1)} copy(bf16[2048,2,2048]{2,0,1:T(8,128)(2,1)} %bitcast.6) | data formatting | bytes 33554432 | tf_op jit(solution)/shard_map/all_to_all | solution.py:36
  606.2 22.8 %convolution_convert_fusion.1 = bf16[1024,2048]{1,0:T(8,128)(2,1)S(1)} fusion(bf16[4096,1024]{0,1:T(8,128)(2,1)} %all-gather.11.cloned.1.call-done, bf16[2048,4096]{0,1:T(8,128)(2,1)} %bitcast.36), kind=kOutput, calls=%fused_computation.7 | convolution fusion | flops 17181966336 | bytes 29360128 | tf_op jit(solution)/shard_map/dot_general | solution.py:37
  629.0 5.6 fusion.12
  634.6 9.4 %copy.40 = f32[2048,1024]{1,0:T(8,128)} copy(f32[2048,1024]{0,1:T(8,128)} %bitcast.34) | data formatting | bytes 16777216
  644.0 161.2 %reduce-scatter.2.cloned.1.call-done = f32[256,2048]{1,0:T(8,128)} async-done(((f32[4096,2048]{1,0:T(8,128)}), f32[256,2048]{1,0:T(8,128)}) %reduce-scatter.2.cloned.1.call-update) | async-done | bytes 2097168 | tf_op jit(solution)/shard_map/reduce_scatter | solution.py:50
  805.2 3.3 multiply_add_fusion.1
  (15 shorter events, 0.2 us)
Async XLA Ops:
  7.2 27.2 %all-gather.5.cloned.1.call-start = ((), (), s32[]{:S(2)}) async-start(), calls=%async_computation.2 | async-start | bytes 1572864 | tf_op jit(solution)/shard_map/all_gather | solution.py:16
  7.9 131.2 %all-gather.7.cloned.1.call-start = ((), (), s32[]{:S(2)}) async-start(), calls=%async_computation.3 | async-start | bytes 12582912 | tf_op jit(solution)/shard_map/all_gather | solution.py:18
  15.3 252.4 %all-gather.9.cloned.1.call-start = ((), (), s32[]{:S(2)}) async-start(), calls=%async_computation.4 | async-start | bytes 17825792 | tf_op jit(solution)/shard_map/all_gather | solution.py:27
  16.0 590.2 %all-gather.11.cloned.1.call-start = ((), (), s32[]{:S(2)}) async-start(), calls=%async_computation.5 | async-start | bytes 12582912 | tf_op jit(solution)/shard_map/all_gather | solution.py:39
  301.5 503.7 %reduce-scatter.2.cloned.1.call-start = ((), (), s32[]{:S(2)}) async-start(), calls=%async_computation.6 | async-start | bytes 35651584 | tf_op jit(solution)/shard_map/reduce_scatter | solution.py:50
  327.3 256.1 %all-to-all-start = ((bf16[2,2048,2048]{2,1,0:T(8,128)(2,1)}), bf16[2,2048,2048]{2,1,0:T(8,128)(2,1)}, u32[]{:S(2)}, u32[]{:S(2)}) async-start(bf16[2,2048,2048]{2,1,0:T(8,128)(2,1)} %bitcast.35), calls=%async_computation | async-start | bytes 33554432 | tf_op jit(solution)/shard_map/all_to_all | solution.py:36
  337.0 7.5 copy-start.2
  606.2 22.8 %copy-start = (bf16[1024,512]{1,0:T(8,128)(2,1)S(1)}, bf16[1024,512]{1,0:T(8,128)(2,1)}, u32[]{:S(2)}) copy-start(bf16[1024,512]{1,0:T(8,128)(2,1)} %all-gather.5.cloned.1.call-done) | copy-start | bytes 3145732
  634.6 170.6 %copy-start.1 = (f32[256,2048]{1,0:T(8,128)S(1)}, f32[256,2048]{1,0:T(8,128)}, u32[]{:S(2)}) copy-start(f32[256,2048]{1,0:T(8,128)} %param.12) | copy-start | bytes 6291460
Sparse Core Ops, SparseCore 0:
  9.5 23.9 all-gather.4
  35.0 103.9 all-gather.6
  141.2 126.4 all-gather.8
  301.6 165.6 all-gather.10
  471.4 333.7 reduce-scatter.1
where the time goes:
time: 816 us; the launch traced here: 815 us
  waiting for transfers between devices  603 us (74%)
  matrix products  107 us (13%)
  local copies, waits for them, and re-layouts  76.7 us (9%)
  between operations  13.8 us (2%)
  starting transfers between devices  10.1 us (1%)
    all_to_all x1, waiting for transfers between devices, local(): lax.all_to_all(left_cols, 'col', split_axis=0, concat_axis=1, tiled=True)  219 us
    reduce_scatter x1, waiting for transfers between devices, local(): lax.psum_scatter(lax.dot_general(gathered, rounded, (((1,), (1,)), ((), (...  161 us
    all_gather x1, waiting for transfers between devices, local(): left_cols = lax.all_gather(left_basis, 'grp', axis=0, tiled=True)  117 us
    all_gather x1, waiting for transfers between devices, local(): gathered = lax.all_gather(rounded, 'col', axis=0, tiled=True)  105 us
    unnamed x12, local copies, waits for them, and re-layouts  53.5 us
    dot_general x1, matrix products, local(): lax.dot_general(left_cols, turned, (((0,), (0,)), ((), ())), preferred_el...  33.8 us
    dot_general x1, matrix products, local(): lax.dot_general(gathered, rounded, (((1,), (1,)), ((), ())), preferred_el...  25.6 us
    all_to_all x1, local copies, waits for them, and re-layouts, local(): lax.all_to_all(left_cols, 'col', split_axis=0, concat_axis=1, tiled=True)  22.8 us
  transfers between devices with their start and end apart: 6, of which 4 were waited for; matrix products, arithmetic and copies ran while one was open for 19% of the time, Pallas kernels for 0%

commit v1 on v0

--- a/solution.py
+++ b/solution.py
@@ -24,7 +24,17 @@
         preferred_element_type=jnp.float32,
     )
     turned = product.reshape(height, cols_here).astype(jnp.bfloat16)
-    left_cols = lax.all_gather(left_basis, "grp", axis=0, tiled=True)
+    sides = [left_basis]
+    workers = lax.psum(1, "grp")
+    m = 0
+    while m < workers - 1:
+        r_now = lax.ppermute(
+            sides[-1], axis_name="grp", perm=[(j0, (j0 + 1) % workers) for j0 in range(workers)]
+        )
+        sides.append(r_now)
+        m = m + 1
+    f_next = jnp.concatenate(sides[::-1], axis=0)
+    left_cols = jnp.roll(f_next, (lax.axis_index("grp") + 1) * left_basis.shape[0], axis=0)
     rotated = lax.dot_general(
         left_cols, turned, (((0,), (0,)), ((), ())), preferred_element_type=jnp.float32
     )

time: 816 us -> 866 us (1.061)
  waiting for transfers between devices: 603 us -> 657 us
    ppermute x0 -> x15, waiting for transfers between devices: none -> 237 us  [local(): lax.ppermute(sides[-1], axis_name='grp', perm=[(j0, (j0 + 1) % workers) f...]
    all_gather x1 -> x0, waiting for transfers between devices: 117 us -> none  [local(): left_cols = lax.all_gather(left_basis, 'grp', axis=0, tiled=True)]
    all_gather x1, waiting for transfers between devices: 105 us -> 0.01 us  [local(): gathered = lax.all_gather(rounded, 'col', axis=0, tiled=True)]
    reduce_scatter x1, waiting for transfers between devices: 161 us -> 184 us  [local(): lax.psum_scatter(lax.dot_general(gathered, rounded, (((1,), (1,)), ((), (...]
    all_to_all x1, waiting for transfers between devices: 219 us -> 237 us  [local(): lax.all_to_all(left_cols, 'col', split_axis=0, concat_axis=1, tiled=True)]
    unnamed x12 -> x69, local copies, waits for them, and re-layouts: 53.5 us -> 39.5 us
  transfers between devices with their start and end apart: 6 -> 20, of which waited for: 4 -> 17; matrix products, arithmetic and copies ran while one was open for 19% -> 13% of each run, Pallas kernels for 0% -> 0%
where the time goes in v1:
time: 866 us; the launch traced here: 865 us
  waiting for transfers between devices  657 us (76%)
  matrix products  109 us (13%)
  local copies, waits for them, and re-layouts  69.5 us (8%)
  between operations  14.2 us (2%)
  starting transfers between devices  10.6 us (1%)
    all_to_all x1, waiting for transfers between devices, local(): lax.all_to_all(left_cols, 'col', split_axis=0, concat_axis=1, tiled=True)  237 us
    ppermute x15, waiting for transfers between devices, local(): lax.ppermute(sides[-1], axis_name='grp', perm=[(j0, (j0 + 1) % workers) f...  237 us
    reduce_scatter x1, waiting for transfers between devices, local(): lax.psum_scatter(lax.dot_general(gathered, rounded, (((1,), (1,)), ((), (...  184 us
    unnamed x69, local copies, waits for them, and re-layouts  39.5 us
    dot_general x1, matrix products, local(): lax.dot_general(left_cols, turned, (((0,), (0,)), ((), ())), preferred_el...  35.4 us
    dot_general x1, matrix products, local(): lax.dot_general(gathered, rounded, (((1,), (1,)), ((), ())), preferred_el...  25.8 us
    dot_general x1, matrix products, local(): jnp.dot(left_rows, lax.all_gather(direction, 'col', axis=0, tiled=True),...  23 us
    all_to_all x1, local copies, waits for them, and re-layouts, local(): lax.all_to_all(left_cols, 'col', split_axis=0, concat_axis=1, tiled=True)  22.6 us
  transfers between devices with their start and end apart: 20, of which 17 were waited for; matrix products, arithmetic and copies ran while one was open for 13% of the time, Pallas kernels for 0%

profile of v1, /device:TPU:0, one launch (start us, length us, event | category | flops | bytes accessed | tf_op | source)
XLA Modules:
  0.0 864.6 jit_solution(6327275457030166406)
XLA Ops:
  7.8 17.7 %collective-permute-done = bf16[256,2048]{1,0:T(8,128)(2,1)S(1)} collective-permute-done((bf16[256,2048]{1,0:T(8,128)(2,1)}, bf16[256,2048]{1,0:T(8,128)(2,1)S(1)}, u32[]{:S(2)}, u32[]{:S(2)}) %collective-permute-start) | collective-permute-done | bytes 1048608 | tf_op jit(solution)/shard_map/ppermute | solution.py:31
  25.4 16.9 %collective-permute-done.1 = bf16[256,2048]{1,0:T(8,128)(2,1)S(1)} collective-permute-done((bf16[256,2048]{1,0:T(8,128)(2,1)S(1)}, bf16[256,2048]{1,0:T(8,128)(2,1)S(1)}, u32[]{:S(2)}, u32[]{:S(2)}) %collective-permute-start.1) | collective-permute-done | bytes 1048608 | tf_op jit(solution)/shard_map/ppermute | solution.py:31
  42.4 16.9 %collective-permute-done.2 = bf16[256,2048]{1,0:T(8,128)(2,1)S(1)} collective-permute-done((bf16[256,2048]{1,0:T(8,128)(2,1)S(1)}, bf16[256,2048]{1,0:T(8,128)(2,1)S(1)}, u32[]{:S(2)}, u32[]{:S(2)}) %collective-permute-start.2) | collective-permute-done | bytes 1048608 | tf_op jit(solution)/shard_map/ppermute | solution.py:31
  59.3 16.9 %collective-permute-done.3 = bf16[256,2048]{1,0:T(8,128)(2,1)S(1)} collective-permute-done((bf16[256,2048]{1,0:T(8,128)(2,1)S(1)}, bf16[256,2048]{1,0:T(8,128)(2,1)S(1)}, u32[]{:S(2)}, u32[]{:S(2)}) %collective-permute-start.3) | collective-permute-done | bytes 1048608 | tf_op jit(solution)/shard_map/ppermute | solution.py:31
  77.2 17.0 %collective-permute-done.4 = bf16[256,2048]{1,0:T(8,128)(2,1)} collective-permute-done((bf16[256,2048]{1,0:T(8,128)(2,1)S(1)}, bf16[256,2048]{1,0:T(8,128)(2,1)}, u32[]{:S(2)}, u32[]{:S(2)}) %collective-permute-start.4) | collective-permute-done | bytes 1048608 | tf_op jit(solution)/shard_map/ppermute | solution.py:31
  94.3 17.2 %collective-permute-done.5 = bf16[256,2048]{1,0:T(8,128)(2,1)} collective-permute-done((bf16[256,2048]{1,0:T(8,128)(2,1)}, bf16[256,2048]{1,0:T(8,128)(2,1)}, u32[]{:S(2)}, u32[]{:S(2)}) %collective-permute-start.5) | collective-permute-done | bytes 1048608 | tf_op jit(solution)/shard_map/ppermute | solution.py:31
  111.4 7.3 copy.24
  118.8 9.8 %collective-permute-done.6 = bf16[256,2048]{1,0:T(8,128)(2,1)} collective-permute-done((bf16[256,2048]{1,0:T(8,128)(2,1)}, bf16[256,2048]{1,0:T(8,128)(2,1)}, u32[]{:S(2)}, u32[]{:S(2)}) %collective-permute-start.6) | collective-permute-done | bytes 1048608 | tf_op jit(solution)/shard_map/ppermute | solution.py:31
  128.7 17.1 %collective-permute-done.7 = bf16[256,2048]{1,0:T(8,128)(2,1)S(1)} collective-permute-done((bf16[256,2048]{1,0:T(8,128)(2,1)}, bf16[256,2048]{1,0:T(8,128)(2,1)S(1)}, u32[]{:S(2)}, u32[]{:S(2)}) %collective-permute-start.7) | collective-permute-done | bytes 1048608 | tf_op jit(solution)/shard_map/ppermute | solution.py:31
  146.8 16.9 %collective-permute-done.8 = bf16[256,2048]{1,0:T(8,128)(2,1)S(1)} collective-permute-done((bf16[256,2048]{1,0:T(8,128)(2,1)S(1)}, bf16[256,2048]{1,0:T(8,128)(2,1)S(1)}, u32[]{:S(2)}, u32[]{:S(2)}) %collective-permute-start.8) | collective-permute-done | bytes 1048608 | tf_op jit(solution)/shard_map/ppermute | solution.py:31
  164.7 16.9 %collective-permute-done.9 = bf16[256,2048]{1,0:T(8,128)(2,1)S(1)} collective-permute-done((bf16[256,2048]{1,0:T(8,128)(2,1)S(1)}, bf16[256,2048]{1,0:T(8,128)(2,1)S(1)}, u32[]{:S(2)}, u32[]{:S(2)}) %collective-permute-start.9) | collective-permute-done | bytes 1048608 | tf_op jit(solution)/shard_map/ppermute | solution.py:31
  182.6 16.9 %collective-permute-done.10 = bf16[256,2048]{1,0:T(8,128)(2,1)S(1)} collective-permute-done((bf16[256,2048]{1,0:T(8,128)(2,1)S(1)}, bf16[256,2048]{1,0:T(8,128)(2,1)S(1)}, u32[]{:S(2)}, u32[]{:S(2)}) %collective-permute-start.10) | collective-permute-done | bytes 1048608 | tf_op jit(solution)/shard_map/ppermute | solution.py:31
  200.5 16.9 %collective-permute-done.11 = bf16[256,2048]{1,0:T(8,128)(2,1)S(1)} collective-permute-done((bf16[256,2048]{1,0:T(8,128)(2,1)S(1)}, bf16[256,2048]{1,0:T(8,128)(2,1)S(1)}, u32[]{:S(2)}, u32[]{:S(2)}) %collective-permute-start.11) | collective-permute-done | bytes 1048608 | tf_op jit(solution)/shard_map/ppermute | solution.py:31
  218.4 16.9 %collective-permute-done.12 = bf16[256,2048]{1,0:T(8,128)(2,1)S(1)} collective-permute-done((bf16[256,2048]{1,0:T(8,128)(2,1)S(1)}, bf16[256,2048]{1,0:T(8,128)(2,1)S(1)}, u32[]{:S(2)}, u32[]{:S(2)}) %collective-permute-start.12) | collective-permute-done | bytes 1048608 | tf_op jit(solution)/shard_map/ppermute | solution.py:31
  236.3 17.0 %collective-permute-done.13 = bf16[256,2048]{1,0:T(8,128)(2,1)} collective-permute-done((bf16[256,2048]{1,0:T(8,128)(2,1)S(1)}, bf16[256,2048]{1,0:T(8,128)(2,1)}, u32[]{:S(2)}, u32[]{:S(2)}) %collective-permute-start.13) | collective-permute-done | bytes 1048608 | tf_op jit(solution)/shard_map/ppermute | solution.py:31
  253.4 11.8 %convolution_convert_fusion = bf16[2,512,4096]{2,1,0:T(8,128)(2,1)} fusion(bf16[2,512,512]{2,1,0:T(8,128)(2,1)} %bitcast.31, bf16[4096,2,512]{0,2,1:T(8,128)(2,1)} %bitcast.33), kind=kOutput, calls=%fused_computation.4 | convolution fusion | flops 4299161600 | bytes 17825792 | tf_op jit(solution)/shard_map/mbj,bjr->mbr/dot_general | solution.py:20
  293.9 35.4 %divide_convert_fusion = (bf16[2048,1024]{1,0:T(8,128)(2,1)}, f32[2048,1024]{1,0:T(8,128)}, f32[2048,1024]{1,0:T(8,128)}) fusion(f32[2048,1024]{1,0:T(8,128)} %param.8, f32[2048,1024]{1,0:T(8,128)} %param.9, bf16[4096,2048]{1,0:T(8,128)(2,1)} %constant_dynamic-slice_fusion, bf16[4096,1024]{0,1:T(8,128)(2,1)} %bitcast.35), kind=kOutput, calls=%fused_computation.3 | convolution fusion | flops 17202937856 | bytes 62914560 | tf_op jit(solution)/shard_map/dot_general | solution.py:38
  329.4 25.8 %fusion.11 = f32[4096,2048]{1,0:T(8,128)} fusion(bf16[4096,1024]{0,1:T(8,128)(2,1)} %all-gather.6.cloned.1.call-done, bf16[2048,1024]{0,1:T(8,128)(2,1)} %copy.24), kind=kOutput, calls=%fused_computation.46 | convolution fusion | flops 17179869184 | bytes 46137344 | tf_op jit(solution)/shard_map/dot_general | solution.py:61
  355.2 9.9 %all-to-all-start = ((bf16[2,2048,2048]{2,1,0:T(8,128)(2,1)}), bf16[2,2048,2048]{2,1,0:T(8,128)(2,1)}, u32[]{:S(2)}, u32[]{:S(2)}) async-start(bf16[2,2048,2048]{2,1,0:T(8,128)(2,1)} %bitcast.27), calls=%async_computation | async-start | bytes 33554432 | tf_op jit(solution)/shard_map/all_to_all | solution.py:46
  373.6 237.2 %all-to-all-done = bf16[2,2048,2048]{2,1,0:T(8,128)(2,1)} async-done(((bf16[2,2048,2048]{2,1,0:T(8,128)(2,1)}), bf16[2,2048,2048]{2,1,0:T(8,128)(2,1)}, u32[]{:S(2)}, u32[]{:S(2)}) %all-to-all-start) | async-done | bytes 16777248 | tf_op jit(solution)/shard_map/all_to_all | solution.py:46
  610.8 22.6 %copy.23 = bf16[2048,2,2048]{0,2,1:T(8,128)(2,1)} copy(bf16[2048,2,2048]{2,0,1:T(8,128)(2,1)} %bitcast.1) | data formatting | bytes 33554432 | tf_op jit(solution)/shard_map/all_to_all | solution.py:46
  633.4 23.0 %convolution_convert_fusion.1 = bf16[2048,1024]{0,1:T(8,128)(2,1)S(1)} fusion(bf16[2048,4096]{0,1:T(8,128)(2,1)} %bitcast.29, bf16[4096,1024]{1,0:T(8,128)(2,1)} %all-gather.8.cloned.1.call-done), kind=kOutput, calls=%fused_computation.7 | convolution fusion | flops 17181966336 | bytes 29360128 | tf_op jit(solution)/shard_map/dot_general | solution.py:47
  662.0 9.2 %copy.30 = f32[2048,1024]{1,0:T(8,128)} copy(f32[2048,1024]{0,1:T(8,128)} %bitcast.28) | data formatting | bytes 16777216
  671.3 183.5 %reduce-scatter.2.cloned.1.call-done = f32[256,2048]{1,0:T(8,128)} async-done(((f32[4096,2048]{1,0:T(8,128)}), f32[256,2048]{1,0:T(8,128)}) %reduce-scatter.2.cloned.1.call-update) | async-done | bytes 2097168 | tf_op jit(solution)/shard_map/reduce_scatter | solution.py:60
  (101 shorter events, 53.5 us)
Async XLA Ops:
  7.2 246.1 %all-gather.4.cloned.1.call-start = ((), (), s32[]{:S(2)}) async-start(), calls=%async_computation.2 | async-start | bytes 1572864 | tf_op jit(solution)/shard_map/all_gather | solution.py:16
  7.2 18.2 %collective-permute-start = (bf16[256,2048]{1,0:T(8,128)(2,1)}, bf16[256,2048]{1,0:T(8,128)(2,1)S(1)}, u32[]{:S(2)}, u32[]{:S(2)}) collective-permute-start(bf16[256,2048]{1,0:T(8,128)(2,1)} %param.10), channel_id=1, source_target_pairs={{0,2},{2,4},{4,6},{6,8},{8,10},{10,12},{12,14},{14,16},{16,18},{18... | collective-permute-start | bytes 3145736 | tf_op jit(solution)/shard_map/ppermute | solution.py:31
  25.4 16.9 %collective-permute-start.1 = (bf16[256,2048]{1,0:T(8,128)(2,1)S(1)}, bf16[256,2048]{1,0:T(8,128)(2,1)S(1)}, u32[]{:S(2)}, u32[]{:S(2)}) collective-permute-start(bf16[256,2048]{1,0:T(8,128)(2,1)S(1)} %collective-permute-done), channel_id=1, source_target_pairs={{0,2},{2,4},{4,6},{6,8},{8,10},{10,12},{12,14},{14,16},{16,18},{18... | collective-permute-start | bytes 3145736 | tf_op jit(solution)/shard_map/ppermute | solution.py:31
  42.4 16.9 %collective-permute-start.2 = (bf16[256,2048]{1,0:T(8,128)(2,1)S(1)}, bf16[256,2048]{1,0:T(8,128)(2,1)S(1)}, u32[]{:S(2)}, u32[]{:S(2)}) collective-permute-start(bf16[256,2048]{1,0:T(8,128)(2,1)S(1)} %collective-permute-done.1), channel_id=1, source_target_pairs={{0,2},{2,4},{4,6},{6,8},{8,10},{10,12},{12,14},{14,16},{16,18},{18... | collective-permute-start | bytes 3145736 | tf_op jit(solution)/shard_map/ppermute | solution.py:31
  59.3 16.9 %collective-permute-start.3 = (bf16[256,2048]{1,0:T(8,128)(2,1)S(1)}, bf16[256,2048]{1,0:T(8,128)(2,1)S(1)}, u32[]{:S(2)}, u32[]{:S(2)}) collective-permute-start(bf16[256,2048]{1,0:T(8,128)(2,1)S(1)} %collective-permute-done.2), channel_id=1, source_target_pairs={{0,2},{2,4},{4,6},{6,8},{8,10},{10,12},{12,14},{14,16},{16,18},{18... | collective-permute-start | bytes 3145736 | tf_op jit(solution)/shard_map/ppermute | solution.py:31
  77.2 17.0 %collective-permute-start.4 = (bf16[256,2048]{1,0:T(8,128)(2,1)S(1)}, bf16[256,2048]{1,0:T(8,128)(2,1)}, u32[]{:S(2)}, u32[]{:S(2)}) collective-permute-start(bf16[256,2048]{1,0:T(8,128)(2,1)S(1)} %collective-permute-done.3), channel_id=1, source_target_pairs={{0,2},{2,4},{4,6},{6,8},{8,10},{10,12},{12,14},{14,16},{16,18},{18... | collective-permute-start | bytes 3145736 | tf_op jit(solution)/shard_map/ppermute | solution.py:31
  94.2 17.2 %collective-permute-start.5 = (bf16[256,2048]{1,0:T(8,128)(2,1)}, bf16[256,2048]{1,0:T(8,128)(2,1)}, u32[]{:S(2)}, u32[]{:S(2)}) collective-permute-start(bf16[256,2048]{1,0:T(8,128)(2,1)} %collective-permute-done.4), channel_id=1, source_target_pairs={{0,2},{2,4},{4,6},{6,8},{8,10},{10,12},{12,14},{14,16},{16,18},{18... | collective-permute-start | bytes 3145736 | tf_op jit(solution)/shard_map/ppermute | solution.py:31
  94.2 159.1 %all-gather.6.cloned.1.call-start = ((), (), s32[]{:S(2)}) async-start(), calls=%async_computation.3 | async-start | bytes 12582912 | tf_op jit(solution)/shard_map/all_gather | solution.py:18
  111.4 17.2 %collective-permute-start.6 = (bf16[256,2048]{1,0:T(8,128)(2,1)}, bf16[256,2048]{1,0:T(8,128)(2,1)}, u32[]{:S(2)}, u32[]{:S(2)}) collective-permute-start(bf16[256,2048]{1,0:T(8,128)(2,1)} %collective-permute-done.5), channel_id=1, source_target_pairs={{0,2},{2,4},{4,6},{6,8},{8,10},{10,12},{12,14},{14,16},{16,18},{18... | collective-permute-start | bytes 3145736 | tf_op jit(solution)/shard_map/ppermute | solution.py:31
  118.8 514.6 %all-gather.8.cloned.1.call-start = ((), (), s32[]{:S(2)}) async-start(), calls=%async_computation.4 | async-start | bytes 12582912 | tf_op jit(solution)/shard_map/all_gather | solution.py:49
  128.7 17.1 %collective-permute-start.7 = (bf16[256,2048]{1,0:T(8,128)(2,1)}, bf16[256,2048]{1,0:T(8,128)(2,1)S(1)}, u32[]{:S(2)}, u32[]{:S(2)}) collective-permute-start(bf16[256,2048]{1,0:T(8,128)(2,1)} %collective-permute-done.6), channel_id=1, source_target_pairs={{0,2},{2,4},{4,6},{6,8},{8,10},{10,12},{12,14},{14,16},{16,18},{18... | collective-permute-start | bytes 3145736 | tf_op jit(solution)/shard_map/ppermute | solution.py:31
  146.8 16.9 %collective-permute-start.8 = (bf16[256,2048]{1,0:T(8,128)(2,1)S(1)}, bf16[256,2048]{1,0:T(8,128)(2,1)S(1)}, u32[]{:S(2)}, u32[]{:S(2)}) collective-permute-start(bf16[256,2048]{1,0:T(8,128)(2,1)S(1)} %collective-permute-done.7), channel_id=1, source_target_pairs={{0,2},{2,4},{4,6},{6,8},{8,10},{10,12},{12,14},{14,16},{16,18},{18... | collective-permute-start | bytes 3145736 | tf_op jit(solution)/shard_map/ppermute | solution.py:31
  164.7 16.9 %collective-permute-start.9 = (bf16[256,2048]{1,0:T(8,128)(2,1)S(1)}, bf16[256,2048]{1,0:T(8,128)(2,1)S(1)}, u32[]{:S(2)}, u32[]{:S(2)}) collective-permute-start(bf16[256,2048]{1,0:T(8,128)(2,1)S(1)} %collective-permute-done.8), channel_id=1, source_target_pairs={{0,2},{2,4},{4,6},{6,8},{8,10},{10,12},{12,14},{14,16},{16,18},{18... | collective-permute-start | bytes 3145736 | tf_op jit(solution)/shard_map/ppermute | solution.py:31
  182.6 16.9 %collective-permute-start.10 = (bf16[256,2048]{1,0:T(8,128)(2,1)S(1)}, bf16[256,2048]{1,0:T(8,128)(2,1)S(1)}, u32[]{:S(2)}, u32[]{:S(2)}) collective-permute-start(bf16[256,2048]{1,0:T(8,128)(2,1)S(1)} %collective-permute-done.9), channel_id=1, source_target_pairs={{0,2},{2,4},{4,6},{6,8},{8,10},{10,12},{12,14},{14,16},{16,18},{18... | collective-permute-start | bytes 3145736 | tf_op jit(solution)/shard_map/ppermute | solution.py:31
  200.5 16.9 %collective-permute-start.11 = (bf16[256,2048]{1,0:T(8,128)(2,1)S(1)}, bf16[256,2048]{1,0:T(8,128)(2,1)S(1)}, u32[]{:S(2)}, u32[]{:S(2)}) collective-permute-start(bf16[256,2048]{1,0:T(8,128)(2,1)S(1)} %collective-permute-done.10), channel_id=1, source_target_pairs={{0,2},{2,4},{4,6},{6,8},{8,10},{10,12},{12,14},{14,16},{16,18},{18... | collective-permute-start | bytes 3145736 | tf_op jit(solution)/shard_map/ppermute | solution.py:31
  218.4 16.9 %collective-permute-start.12 = (bf16[256,2048]{1,0:T(8,128)(2,1)S(1)}, bf16[256,2048]{1,0:T(8,128)(2,1)S(1)}, u32[]{:S(2)}, u32[]{:S(2)}) collective-permute-start(bf16[256,2048]{1,0:T(8,128)(2,1)S(1)} %collective-permute-done.11), channel_id=1, source_target_pairs={{0,2},{2,4},{4,6},{6,8},{8,10},{10,12},{12,14},{14,16},{16,18},{18... | collective-permute-start | bytes 3145736 | tf_op jit(solution)/shard_map/ppermute | solution.py:31
  236.3 17.0 %collective-permute-start.13 = (bf16[256,2048]{1,0:T(8,128)(2,1)S(1)}, bf16[256,2048]{1,0:T(8,128)(2,1)}, u32[]{:S(2)}, u32[]{:S(2)}) collective-permute-start(bf16[256,2048]{1,0:T(8,128)(2,1)S(1)} %collective-permute-done.12), channel_id=1, source_target_pairs={{0,2},{2,4},{4,6},{6,8},{8,10},{10,12},{12,14},{14,16},{16,18},{18... | collective-permute-start | bytes 3145736 | tf_op jit(solution)/shard_map/ppermute | solution.py:31
  253.3 17.2 %collective-permute-start.14 = (bf16[256,2048]{1,0:T(8,128)(2,1)}, bf16[256,2048]{1,0:T(8,128)(2,1)}, u32[]{:S(2)}, u32[]{:S(2)}) collective-permute-start(bf16[256,2048]{1,0:T(8,128)(2,1)} %collective-permute-done.13), channel_id=1, source_target_pairs={{0,2},{2,4},{4,6},{6,8},{8,10},{10,12},{12,14},{14,16},{16,18},{18... | collective-permute-start | bytes 3145736 | tf_op jit(solution)/shard_map/ppermute | solution.py:31
  253.3 25.6 %copy-start.2 = (bf16[256,2048]{1,0:T(8,128)(2,1)S(1)}, bf16[256,2048]{1,0:T(8,128)(2,1)}, u32[]{:S(2)}) copy-start(bf16[256,2048]{1,0:T(8,128)(2,1)} %copy-done.1) | copy-start | bytes 3145732
  253.4 25.9 %copy-start = (bf16[256,2048]{1,0:T(8,128)(2,1)S(1)}, bf16[256,2048]{1,0:T(8,128)(2,1)}, u32[]{:S(2)}) copy-start(bf16[256,2048]{1,0:T(8,128)(2,1)} %param.10) | copy-start | bytes 3145732
  329.3 525.5 %reduce-scatter.2.cloned.1.call-start = ((), (), s32[]{:S(2)}) async-start(), calls=%async_computation.5 | async-start | bytes 35651584 | tf_op jit(solution)/shard_map/reduce_scatter | solution.py:60
  355.2 255.6 %all-to-all-start = ((bf16[2,2048,2048]{2,1,0:T(8,128)(2,1)}), bf16[2,2048,2048]{2,1,0:T(8,128)(2,1)}, u32[]{:S(2)}, u32[]{:S(2)}) async-start(bf16[2,2048,2048]{2,1,0:T(8,128)(2,1)} %bitcast.27), calls=%async_computation | async-start | bytes 33554432 | tf_op jit(solution)/shard_map/all_to_all | solution.py:46
  633.4 23.0 %copy-start.15 = (bf16[1024,512]{1,0:T(8,128)(2,1)S(1)}, bf16[1024,512]{1,0:T(8,128)(2,1)}, u32[]{:S(2)}) copy-start(bf16[1024,512]{1,0:T(8,128)(2,1)} %all-gather.4.cloned.1.call-done) | copy-start | bytes 3145732
  656.4 198.4 %copy-start.16 = (f32[256,2048]{1,0:T(8,128)S(1)}, f32[256,2048]{1,0:T(8,128)}, u32[]{:S(2)}) copy-start(f32[256,2048]{1,0:T(8,128)} %param.12) | copy-start | bytes 6291460
  (14 other events, 147.6 us)
Sparse Core Ops, SparseCore 0:
  94.3 22.8 all-gather.3
  118.9 105.5 all-gather.5
  329.4 173.0 all-gather.7
  506.6 348.1 reduce-scatter.1
